TPU v7x, 32 devices: a whole 2x2x4 slice. The times are simulated.
32 devices in a mesh: row: 8 (over z, x), col: 4 (over y, core).
Axes of the slice: x: 2, y: 2, z: 4, core: 2. Of those that a mesh axis runs over, the one named last changes fastest.
Arguments:
- eigvecs: float32 [2048, 512], P('row', 'col'), may hold values from -6 to 6
- reflectors: float32 [8, 32, 128, 64], P(None, ('row', 'col')), may hold values from -2 to 2, as said below
- factors: float32 [8, 32, 64, 64], P(None, ('row', 'col')), may hold values from -3 to 3, as said below
- order: int32 [8], replicated, may hold values from 0 to 7, each once
- offsets: int32 [8], replicated, may hold values from 0 to 63
Outputs:
- rotated: float32 [2048, 512], P('row', 'col')
Inputs may be any that keep to these rules, and one draw needn't show every extreme that they name: `order`: a permutation of 0 .. 7. Every block map is orthogonal: with V the block of reflectors and T the block of factors, T is upper triangular and T^-1 + T^-T = V^T V. `factors`: upper triangular, paired with reflectors as promised there.
All inputs are finite; a program needn't handle non-finite values.
Results may differ from a plain program's by a relative error of at most 0.0003.
Values sent between devices are 32-bit elements; how exact they have to be, the bound alone decides.
A program may use at most 64 MiB of HBM per device.

v0:
```python
import functools

import jax
import jax.numpy as jnp
from jax import lax
from jax.experimental import pallas as pl
from jax.experimental.pallas import tpu as pltpu
from jax.sharding import PartitionSpec as P

MESH = pl.DeviceIdType.MESH
highest = lax.Precision.HIGHEST


def split(x):
    hi = x.astype(jnp.bfloat16)
    lo = (x - hi.astype(jnp.float32)).astype(jnp.bfloat16)
    return hi, lo


def product(a, b):
    a_hi, a_lo = split(a)
    b_hi, b_lo = split(b)
    dot = functools.partial(jnp.dot, preferred_element_type=jnp.float32)
    return dot(a_hi, b_hi) + (dot(a_hi, b_lo) + dot(a_lo, b_hi))


def kernel(
    rows_n, cols_n, order_ref, off_ref, x_ref, house_ref, tri_ref, out_ref,
    maps, frames, up_in, down_in, down_out, last_in, response,
    map_send, map_recv, extra_send, extra_recv,
    up_send, up_recv, down_send, down_recv, last_send, last_recv,
):
    row, col = lax.axis_index("row"), lax.axis_index("col")
    sweeps, span = maps.shape[1], maps.shape[2]
    pairs = sweeps // 2
    width = span // 2
    height, columns = x_ref.shape
    per = height // width
    pad = span
    first = row == 0
    above, below = row > 0, row < rows_n - 1
    odd = lax.rem(col, 2)
    near = col + 1 - 2 * odd
    far = lax.rem(col + cols_n // 2, cols_n)
    low = col < 2

    def send(src, dst, sent, got, to_row, to_col):
        return pltpu.make_async_remote_copy(
            src_ref=src, dst_ref=dst, send_sem=sent, recv_sem=got,
            device_id=(to_row, to_col), device_id_type=MESH,
        )

    def map_copy(kind, p):
        slot = far if kind == 2 else col
        place = maps.at[slot, p]
        to = far if kind == 1 else near
        return send(place, place, map_send.at[kind, p], map_recv.at[slot, p], row, to)

    def map_arrival(j, p):
        return send(maps.at[j, p], maps.at[j, p], map_send.at[0, p], map_recv.at[j, p], row, near)

    def extra_up(t):
        return send(
            maps.at[col, 2 * t], maps.at[cols_n + odd, 2 * t],
            extra_send.at[0, t], extra_recv.at[odd, t], row - 1, col,
        )

    def extra_copy(kind, t, slot):
        place = maps.at[cols_n + slot, 2 * t]
        to = far if kind == 2 else near
        return send(place, place, extra_send.at[kind, t], extra_recv.at[slot, t], row, to)

    def up_copy(t, part, src):
        return send(
            src, up_in.at[t, part], up_send.at[t, part], up_recv.at[t, part], row - 1, col
        )

    def down_copy(q):
        return send(
            down_out.at[q], down_in.at[q], down_send.at[q], down_recv.at[q], row + 1, col
        )

    def last_copy():
        return send(
            frames.at[sweeps, pl.ds(pad + height - width, width)], last_in,
            last_send, last_recv, row + 1, col,
        )

    barrier = pltpu.get_barrier_semaphore()

    def greet(to_row, to_col):
        pl.semaphore_signal(
            barrier, inc=1, device_id=(to_row, to_col), device_id_type=MESH
        )

    greet(row, near)
    greet(row, far)

    @pl.when(above)
    def _():
        greet(row - 1, col)

    @pl.when(below)
    def _():
        greet(row + 1, col)

    def dense(p):
        house = house_ref[order_ref[p], 0]
        tri = tri_ref[order_ref[p], 0]
        scaled = jnp.dot(tri, house, precision=highest, preferred_element_type=jnp.float32)
        inner = lax.dot_general(
            house, scaled, (((0,), (0,)), ((), ())), precision=highest,
            preferred_element_type=jnp.float32,
        )
        eye = lax.broadcasted_iota(jnp.int32, inner.shape, 0) == lax.broadcasted_iota(
            jnp.int32, inner.shape, 1
        )
        maps[col, p] = jnp.where(eye, 1.0, 0.0) - inner

    dense(0)
    frames[0, pl.ds(pad, height), :] = x_ref[...]
    greeted = 2 + jnp.minimum(row, 1) + jnp.minimum(rows_n - 1 - row, 1)
    pl.semaphore_wait(barrier, greeted)
    map_copy(1, 0).start()
    map_copy(0, 0).start()

    @pl.when(above)
    def _():
        for part in range(per):
            up_copy(0, part, x_ref.at[pl.ds(part * width, width)]).start()

    @pl.when(above & low)
    def _():
        extra_up(0).start()

    def spread(p, _):
        dense(p)
        map_copy(1, p).start()
        map_copy(0, p).start()

        @pl.when(above & low & (lax.rem(p, 2) == 0))
        def _():
            extra_up(p // 2).start()

        return 0

    def relay(t):
        for q in (2 * t, 2 * t + 1):
            map_arrival(far, q).wait_recv()
            map_copy(2, q).start()

        @pl.when(below)
        def _():
            extra_copy(1, t, odd).wait_recv()
            extra_copy(1, t, odd).start()

            @pl.when(low)
            def _():
                extra_copy(2, t, odd).start()

    lax.fori_loop(1, sweeps, spread, 0)
    relay(0)

    blank = jnp.zeros((width, columns), jnp.float32)

    def pair(t, _):
        a, b = 2 * t, 2 * t + 1
        start_a, start_b = off_ref[order_ref[a]], off_ref[order_ref[b]]
        before = jnp.where(t == 0, 0, off_ref[order_ref[jnp.maximum(a - 1, 0)]])
        shift = {0: start_a - before, 1: start_b - start_a}
        start = {0: start_a, 1: start_b}
        for q in (a, b):
            for j in range(cols_n):

                @pl.when((col != j) & (far != j))
                def _(j=j, q=q):
                    map_arrival(j, q).wait_recv()

        @pl.when(below)
        def _():
            extra_copy(1, t, 1 - odd).wait_recv()

        def fresh(n, j):
            rows = frames[a + n, pl.ds(pad + (j + 1) * width + shift[n], width), :]
            index = row * height + (j + 1) * width + start[n]
            index = index + lax.broadcasted_iota(jnp.int32, rows.shape, 0)
            return jnp.where(index < rows_n * height, rows, 0.0)

        def early(n, j):
            return product(maps[j, a + n], jnp.concatenate([blank, fresh(n, j)], 0))

        def late(n, j, ready, carried):
            return ready + product(maps[j, a + n], jnp.concatenate([carried, blank], 0))

        def put(n, j, value):
            frames[a + n + 1, pl.ds(pad + j * width, width), :] = value

        def arrive(part):
            @pl.when(below)
            def _():
                up_copy(t, part, up_in.at[t, part]).wait_recv()

            frames[a, pl.ds(pad + height + part * width, width), :] = up_in[t, part]

        def lead(n):
            put(n, -1, frames[a + n, pl.ds(pad - width + shift[n], width), :])
            return frames[a + n, pl.ds(pad + shift[n], width), :]

        def entry(n, own):
            @pl.when(above)
            def _():
                down_copy(a + n).wait_recv()

            return jnp.where(first, own, down_in[a + n])

        def leave(n, carried):
            down_out[a + n] = carried

            @pl.when(below)
            def _():
                down_copy(a + n).start()

        def lift(part):
            @pl.when(above & (t < pairs - 1))
            def _():
                place = frames.at[a + 2, pl.ds(pad + part * width, width)]
                up_copy(t + 1, part, place).start()

        def respond(n):
            block = maps[0, a + n][:, :width]
            for j in range(per):
                if j:
                    block = product(maps[j, a + n][:, :width], block[width:])
                response[n, pl.ds(j * width, width), :] = block[:width]
            response[n, pl.ds(per * width, width), :] = block[width:]

        def idle(n, j, carried):
            ready = early(n, j)
            if carried is not None:
                ready = late(n, j, ready, carried)
            return ready

        def settle(n, parts, own):
            whole = jnp.concatenate(parts, 0) + product(response[n], entry(n, own))
            for j in range(per):
                put(n, j, whole[j * width : (j + 1) * width])
            carried = whole[per * width :]
            leave(n, carried)
            return carried

        respond(0)
        respond(1)
        parts, carried = [], None
        own = lead(0)
        for j in range(per):
            if j >= per - 2:
                arrive(j - (per - 2))
            both = idle(0, j, carried)
            parts.append(both[:width])
            carried = both[width:]
        carried = settle(0, parts + [carried], own)

        @pl.when(t < pairs - 1)
        def _():
            relay(t + 1)

        own = lead(1)
        arrive(2)
        arrive(3)
        parts, other = [], None
        for j in range(per):
            if j < 2:
                both = late(0, per + j, early(0, per + j), carried)
                put(0, per + j, both[:width])
                carried = both[width:]
            both = idle(1, j, other)
            parts.append(both[:width])
            other = both[width:]
        settle(1, parts + [other], own)
        for j in range(per):
            lift(j)
        return 0

    lax.fori_loop(0, pairs, pair, 0)

    @pl.when(below)
    def _():
        last_copy().start()

    @pl.when(above)
    def _():
        last_copy().wait_recv()

    edge = frames[sweeps, pl.ds(pad - width, width), :]
    frames[sweeps, pl.ds(pad - width, width), :] = jnp.where(first, edge, last_in[...])
    shift_back = off_ref[order_ref[sweeps - 1]]
    out_ref[...] = frames[sweeps, pl.ds(pad - shift_back, height), :]

    def drain(t, _):
        for q in (2 * t, 2 * t + 1):
            for kind in range(3):
                map_copy(kind, q).wait_send()

            @pl.when(below)
            def _(q=q):
                down_copy(q).wait_send()

        @pl.when(above)
        def _():
            for part in range(per):
                up_copy(t, part, up_in.at[t, part]).wait_send()

            @pl.when(low)
            def _():
                extra_up(t).wait_send()

        @pl.when(below)
        def _():
            extra_copy(1, t, odd).wait_send()

            @pl.when(low)
            def _():
                extra_copy(2, t, odd).wait_send()

        return 0

    lax.fori_loop(0, pairs, drain, 0)

    @pl.when(below)
    def _():
        last_copy().wait_send()


def local(rows_n, cols_n, eigvecs, reflectors, factors, order, offsets):
    sweeps, _, span, width = reflectors.shape
    height, columns = eigvecs.shape
    part = (width, columns)
    vmem = pl.BlockSpec(memory_space=pltpu.VMEM)
    smem = pl.BlockSpec(memory_space=pltpu.SMEM)
    dma = pltpu.SemaphoreType.DMA
    return pl.pallas_call(
        functools.partial(kernel, rows_n, cols_n),
        out_shape=jax.ShapeDtypeStruct((height, columns), jnp.float32),
        in_specs=[smem, smem, vmem, vmem, vmem],
        out_specs=vmem,
        scratch_shapes=[
            pltpu.VMEM((cols_n + 2, sweeps, span, span), jnp.float32),
            pltpu.VMEM((sweeps + 1, 2 * height + span, columns), jnp.float32),
            pltpu.VMEM((sweeps // 2, height // width) + part, jnp.float32),
            pltpu.VMEM((sweeps,) + part, jnp.float32),
            pltpu.VMEM((sweeps,) + part, jnp.float32),
            pltpu.VMEM(part, jnp.float32),
            pltpu.VMEM((2, height + width, width), jnp.float32),
            dma((3, sweeps)),
            dma((cols_n, sweeps)),
            dma((3, sweeps // 2)),
            dma((2, sweeps // 2)),
            dma((sweeps // 2, height // width)),
            dma((sweeps // 2, height // width)),
            dma((sweeps,)),
            dma((sweeps,)),
            dma,
            dma,
        ],
        compiler_params=pltpu.CompilerParams(collective_id=0, has_side_effects=True),
    )(order, offsets, eigvecs, jnp.swapaxes(reflectors, 2, 3), factors)


def solution(mesh):
    placed = (
        P("row", "col"),
        P(None, ("row", "col"), None, None),
        P(None, ("row", "col"), None, None),
        P(),
        P(),
    )
    body = functools.partial(local, mesh.shape["row"], mesh.shape["col"])
    return jax.shard_map(
        body, mesh=mesh, in_specs=placed, out_specs=P("row", "col"), check_vma=False
    )
```

profile of v0, /device:TPU:30, one launch (start us, length us, event | category | flops | bytes accessed | tf_op | source)
XLA Modules:
  0.0 75.8 jit_solution(1711045792607231400)
XLA Ops:
  0.0 74.2 %shard_map.55 = f32[256,128]{1,0:T(8,128)} custom-call(s32[8]{0:T(128)} %order_ref.1, s32[8]{0:T(128)} %off_ref.1, f32[256,128]{1,0:T(8,128)} %x_ref.1, f32[8,1,64,128]{3,2,1,0:T(8,128)} %bitcast.1, f32[8,1,64,64]{3,2,1,0:T(8,128)} %tri_ref.1), custom_call_target="tpu_custom_call" | custom-call | tf_op jit(solution)/shard_map/pallas_call | solution.py:341
  74.2 1.6 %copy.7 = f32[256,128]{1,0:T(8,128)} copy(f32[256,128]{1,0:T(8,128)} %shard_map.55) | data formatting | bytes 262144
where the time goes:
time: 76 us; the launch traced here: 75.8 us
  Pallas kernels  74.2 us (98%)
  local copies, waits for them, and re-layouts  1.57 us (2%)
    pallas_call x1, Pallas kernels, local(): pl.pallas_call(functools.partial(kernel, rows_n, cols_n), out_shape=jax.S...  74.2 us
    unnamed x1, local copies, waits for them, and re-layouts  1.57 us

commit v1 on v0

v1 whole, which is shorter than its diff:
```python
import functools

import jax
import jax.numpy as jnp
from jax import lax
from jax.experimental import pallas as pl
from jax.experimental.pallas import tpu as pltpu
from jax.sharding import PartitionSpec as P

MESH = pl.DeviceIdType.MESH
SKEW = 2
FORWARD_LEAD = 1
APPLY_LEAD = 5
CHUNK = 2


def split(x):
    hi = x.astype(jnp.bfloat16)
    lo = (x - hi.astype(jnp.float32)).astype(jnp.bfloat16)
    return hi, lo


def dot(a, b, dims=((1,), (0,))):
    return lax.dot_general(a, b, (dims, ((), ())), preferred_element_type=jnp.float32)


def product(a, b, dims=((1,), (0,))):
    (a_hi, a_lo), (b_hi, b_lo) = a, b
    return dot(a_hi, b_hi, dims) + (dot(a_hi, b_lo, dims) + dot(a_lo, b_hi, dims))


def shape_of_planes(rows_n, per, sweeps):
    planes = rows_n // 2
    own = 2 * per
    total = rows_n * per
    starts = [0] + [own * g + SKEW for g in range(1, planes)] + [total + sweeps - 1]
    most = 0
    for g in range(planes):
        begin, wide = starts[g], starts[g + 1] - starts[g]
        for u in range(wide + sweeps - 1):
            live = [
                a for a in range(wide)
                if 0 <= u - a < sweeps and 0 <= begin + 2 * a - u < total
            ]
            most = max(most, len(live))
    widest = max(starts[g + 1] - starts[g] for g in range(planes))
    return planes, own, total, widest, most


def kernel(
    rows_n, cols_n, order_ref, off_ref, x_ref, house_ref, tri_ref, out_ref,
    pack, stage, map_hi, map_lo, state, turned, final,
    arrive, beside, send_x, send_y, send_b, send_z,
    tile_send, tile_recv, carry_send, carry_recv, last_send, last_recv,
):
    row, col = lax.axis_index("row"), lax.axis_index("col")
    sweeps, _, width, span = house_ref.shape
    height, columns = x_ref.shape
    per = height // span
    half = columns // 2
    planes, own, total, widest, most = shape_of_planes(rows_n, per, sweeps)
    spare = state.shape[0] - 1
    plane, side = lax.div(row, 2), lax.rem(row, 2)
    pair, core = lax.div(col, 2), lax.rem(col, 2)
    row_x, col_y, col_b = row + 1 - 2 * side, lax.rem(col + cols_n // 2, cols_n), col + 1 - 2 * core
    top, bottom = plane == 0, plane == planes - 1

    def start_of(g):
        return jnp.where(g == 0, 0, own * g + SKEW)

    def end_of(g):
        return jnp.where(g == planes - 1, total + sweeps - 1, own * (g + 1) + SKEW)

    def plane_of(s):
        return jnp.minimum(lax.div(jnp.maximum(s - SKEW, 0), own), planes - 1)

    begin = start_of(plane)
    wide = end_of(plane) - begin
    steps = jnp.where(top, jnp.minimum(2 * wide - 1, wide + sweeps - 1), wide + sweeps - 1)

    def lowest(u):
        return jnp.maximum(
            jnp.maximum(u - (sweeps - 1), 0), lax.div(jnp.maximum(u - begin + 1, 0), 2)
        )

    def highest_of(u):
        return jnp.minimum(jnp.minimum(u, wide - 1), lax.div(total - 1 - begin + u, 2))

    def remote(src, dst, sent, got, to_row, to_col):
        return pltpu.make_async_remote_copy(
            src_ref=src, dst_ref=dst, send_sem=sent, recv_sem=got,
            device_id=(to_row, to_col), device_id_type=MESH,
        )

    barrier = pltpu.get_barrier_semaphore()
    greeted = 2
    for to_col in (col_y, col_b):
        pl.semaphore_signal(barrier, inc=1, device_id=(row, to_col), device_id_type=MESH)
    for far in range(-2, 3):
        for x in range(2):
            to_row = 2 * (plane + far) + x
            valid = (to_row >= 0) & (to_row < rows_n) & (to_row != row)
            greeted = greeted + jnp.where(valid, 1, 0)

            @pl.when(valid)
            def _(to_row=to_row):
                pl.semaphore_signal(barrier, inc=1, device_id=(to_row, col), device_id_type=MESH)

    mine = row * per + pair

    def lay_out(p):
        s = mine + p
        g = plane_of(s)
        a = s - start_of(g)
        stored = order_ref[p]
        shift = off_ref[stored] + width * core
        house = pltpu.roll(house_ref[stored, 0], shift, 1)
        tri = tri_ref[stored, 0].T
        packed = jnp.concatenate([tri[: width // 2], tri[width // 2 :]], 1)

        @pl.when(g == plane)
        def _():
            pack[a, p, core, pl.ds(0, width), :] = house
            pack[a, p, core, pl.ds(width, width // 2), :] = packed

        @pl.when(g != plane)
        def _():
            stage[p, pl.ds(0, width), :] = house
            stage[p, pl.ds(width, width // 2), :] = packed

    for p in range(sweeps):
        lay_out(p)

    def move(p, act):
        s = mine + p
        g = plane_of(s)
        a = s - start_of(g)

        @pl.when(g != plane)
        def _():
            act(remote(
                stage.at[p], pack.at[a, p, core], send_z.at[p], arrive.at[a, p],
                2 * g + side, col,
            ))

    def hand_out(t, h, act, keep):
        tile = row * per + t
        g = plane_of(jnp.maximum(tile - 1, 0))
        slot = tile - start_of(g) + sweeps - 1
        to_row = 2 * g + h

        @pl.when(to_row != row)
        def _():
            act(remote(
                turned.at[t, pl.ds(h * half, half)], state.at[slot],
                tile_send.at[t, h], tile_recv.at[slot], to_row, col,
            ))

        if keep:
            @pl.when(to_row == row)
            def _():
                state[slot] = turned[t, pl.ds(h * half, half), :]

    for t in range(per):
        turned[t] = x_ref[pl.ds(t * span, span), :].T

    @pl.when(bottom)
    def _():
        state[total - begin + sweeps - 1] = jnp.zeros((half, span), jnp.float32)

    pl.semaphore_wait(barrier, greeted)
    for p in range(sweeps):
        move(p, lambda c: c.start())
    for t in range(per):
        for h in range(2):
            hand_out(t, h, lambda c: c.start(), True)

    def route(a, p):
        j = begin + a - p
        home_row = lax.div(j, per)
        same_x = side == lax.rem(home_row, 2)
        same_y = pair == lax.rem(j, per)
        native = lax.div(home_row, 2) == plane
        source = same_x & same_y
        by_x = lax.rem(p, 2) == 0
        waits = jnp.logical_not(source & native)
        to_x = source | (same_x & jnp.logical_not(same_y) & jnp.logical_not(by_x))
        to_y = source | (jnp.logical_not(same_x) & same_y & by_x)
        return waits, to_x, to_y

    def copies(a, p):
        place = pack.at[a, p, core]
        return (
            remote(place, place, send_x.at[a, p], arrive.at[a, p], row_x, col),
            remote(place, place, send_y.at[a, p], arrive.at[a, p], row, col_y),
            remote(place, place, send_b.at[a, p], beside.at[a, p], row, col_b),
        )

    def each(u, act):
        low, high = lowest(u), highest_of(u)

        def one(a, _):
            act(a, u - a)
            return 0

        lax.fori_loop(low, high + 1, one, 0)

    def forward(a, p):
        waits, to_x, to_y = route(a, p)
        by_x, by_y, by_b = copies(a, p)

        @pl.when(waits)
        def _():
            by_x.wait_recv()

        @pl.when(to_x)
        def _():
            by_x.start()

        @pl.when(to_y)
        def _():
            by_y.start()

        by_b.start()

    def settle(a, p):
        _, to_x, to_y = route(a, p)
        by_x, by_y, by_b = copies(a, p)

        @pl.when(to_x)
        def _():
            by_x.wait_send()

        @pl.when(to_y)
        def _():
            by_y.wait_send()

        by_b.wait_send()

    def others(a, p):
        place = pack.at[a, p, 1 - core]
        remote(place, place, send_b.at[a, p], beside.at[a, p], row, col_b).wait_recv()

    lane = lax.broadcasted_iota(jnp.int32, (width, span), 1)
    down = lax.broadcasted_iota(jnp.int32, (span, span), 0)
    across = lax.broadcasted_iota(jnp.int32, (span, span), 1)
    eye = jnp.where(down == across, 1.0, 0.0)

    def tri_of(packed):
        return jnp.concatenate([packed, pltpu.roll(packed, width, 1)], 0)[:, :width]

    def compose(a, p):
        offset = off_ref[order_ref[p]]
        v_a, v_b = pack[a, p, 0, pl.ds(0, width), :], pack[a, p, 1, pl.ds(0, width), :]
        t_a = split(tri_of(pack[a, p, 0, pl.ds(width, width // 2), :]))
        t_b = split(tri_of(pack[a, p, 1, pl.ds(width, width // 2), :]))
        shared = ((lane - offset - width) & (span - 1)) < width
        in_a, in_b = lane >= offset, lane >= offset + width
        s_a, s_b = split(v_a), split(v_b)
        lap = product(split(jnp.where(shared, v_a, 0.0)), s_b, ((1,), (1,)))
        f_b = product(t_b, s_b)
        f_a = product(t_a, s_a)
        e = product(t_a, split(lap))
        ef = product(split(e), split(f_b))
        left = jnp.concatenate([
            jnp.where(in_a, f_a, 0.0) - jnp.where(in_b, ef, 0.0), jnp.where(in_b, f_b, 0.0)
        ], 0)
        right = jnp.concatenate([
            jnp.where(in_a, 0.0, f_a) - jnp.where(in_b, 0.0, ef), jnp.where(in_b, 0.0, f_b)
        ], 0)
        tall = jnp.concatenate([v_a, v_b], 0).T
        inside = down >= jnp.where(across < width, offset, offset + width)
        u = jnp.concatenate([jnp.where(inside, tall, 0.0), jnp.where(inside, 0.0, tall)], 0)
        w = jnp.concatenate([left, right], 1)
        low = product(split(u), split(w))
        unit = jnp.concatenate([
            jnp.concatenate([eye, jnp.zeros_like(eye)], 1),
            jnp.concatenate([jnp.zeros_like(eye), eye], 1),
        ], 0)
        return split(unit - low)

    def form(u):
        low, high = lowest(u), highest_of(u)

        def some(q, _):
            spots = [jnp.minimum(low + q * CHUNK + i, high) for i in range(CHUNK)]
            made = [compose(a, u - a) for a in spots]
            for a, (hi, lo) in zip(spots, made):
                map_hi[a, u - a] = hi
                map_lo[a, u - a] = lo
            return 0

        lax.fori_loop(0, lax.div(high - low + CHUNK, CHUNK), some, 0)

    def carry(p, slot):
        return remote(
            state.at[slot], state.at[sweeps - 1 - p], carry_send.at[p], carry_recv.at[p],
            row + 2, col,
        )

    def finish(a, act, keep):
        j = begin + a - (sweeps - 1)
        to_row = lax.div(j, per)
        t = lax.rem(j, per)
        place = pl.ds(side * half, half)

        @pl.when(to_row != row)
        def _():
            act(remote(
                state.at[a], final.at[t, place], last_send.at[a], last_recv.at[t, side],
                to_row, col,
            ))

        if keep:
            @pl.when(to_row == row)
            def _():
                final[t, place, :] = state[a]

    def lasts(u):
        a = u - (sweeps - 1)
        return (a >= 0) & (a == lowest(u)) & (a <= highest_of(u))

    def passes(u):
        return (highest_of(u) == wide - 1) & (lowest(u) <= wide - 1) & jnp.logical_not(bottom)

    def spills(u):
        p = u - wide + 1
        return passes(u) & (begin + wide - 1 - p == 0) & (p < sweeps - 1)

    def apply(u):
        low, high = lowest(u), highest_of(u)
        tile = begin + u + 1

        @pl.when((u < wide) & (tile < total) & (lax.div(tile, per) != row))
        def _():
            remote(
                state.at[u + sweeps], state.at[u + sweeps], tile_send.at[0, 0],
                tile_recv.at[u + sweeps], row_x, col,
            ).wait_recv()

        @pl.when(top & (u == 0) & (row != 0))
        def _():
            remote(
                state.at[sweeps - 1], state.at[sweeps - 1], tile_send.at[0, 0],
                tile_recv.at[sweeps - 1], row_x, col,
            ).wait_recv()

        @pl.when((low == 0) & jnp.logical_not(top))
        def _():
            carry(u, sweeps - 1 - u).wait_recv()

        def some(count):
            ready = []
            for i in range(count):
                a = low + i
                p = u - a
                x = jnp.concatenate([state[a - p + sweeps - 1], state[a - p + sweeps]], 1)
                ready.append((a, p, x, map_hi[a, p], map_lo[a, p]))
            made = []
            for a, p, x, hi, lo in ready:
                x_hi, x_lo = split(x)
                both = dot(jnp.concatenate([x_hi, x_lo], 0), hi)
                made.append((a, p, both[:half] + (both[half:] + dot(x_hi, lo))))
            for a, p, y in made:
                state[a - p + sweeps - 1] = y[:, :span]
                to = jnp.where(begin + a - p == total - 1, spare, a - p + sweeps)
                state[to] = y[:, span:]

        for count in range(1, most + 1):
            @pl.when(high - low + 1 == count)
            def _(count=count):
                some(count)

        @pl.when(passes(u))
        def _():
            p = u - wide + 1
            carry(p, wide - 1 - p + sweeps).start()

        @pl.when(spills(u))
        def _():
            p = u - wide + 1
            carry(p + 1, wide - 1 - p + sweeps - 1).start()

        @pl.when(lasts(u))
        def _():
            finish(u - (sweeps - 1), lambda c: c.start(), True)

    lead = jnp.minimum(FORWARD_LEAD + APPLY_LEAD * plane, steps)

    def main(v, _):
        @pl.when(v < steps)
        def _():
            each(v, forward)

        w = v - FORWARD_LEAD

        @pl.when((w >= 0) & (w < steps))
        def _():
            each(w, others)
            form(w)

        u = v - lead

        @pl.when(u >= 0)
        def _():
            apply(u)

        return 0

    lax.fori_loop(0, steps + lead, main, 0)

    def drain(u, _):
        each(u, settle)

        @pl.when(passes(u))
        def _():
            p = u - wide + 1
            carry(p, wide - 1 - p + sweeps).wait_send()

        @pl.when(spills(u))
        def _():
            p = u - wide + 1
            carry(p + 1, wide - 1 - p + sweeps - 1).wait_send()

        @pl.when(lasts(u))
        def _():
            finish(u - (sweeps - 1), lambda c: c.wait_send(), False)

        return 0

    lax.fori_loop(0, steps, drain, 0)
    for p in range(sweeps):
        move(p, lambda c: c.wait_send())
    for t in range(per):
        for h in range(2):
            hand_out(t, h, lambda c: c.wait_send(), False)
    for t in range(per):
        g = plane_of(row * per + t + sweeps - 1)
        for h in range(2):
            @pl.when(2 * g + h != row)
            def _(t=t, h=h):
                place = final.at[t, pl.ds(h * half, half)]
                remote(
                    place, place, last_send.at[0], last_recv.at[t, h], row_x, col
                ).wait_recv()

        out_ref[pl.ds(t * span, span), :] = final[t].T


def local(rows_n, cols_n, eigvecs, reflectors, factors, order, offsets):
    sweeps, _, span, width = reflectors.shape
    height, columns = eigvecs.shape
    per = height // span
    _, _, _, widest, _ = shape_of_planes(rows_n, per, sweeps)
    slots = widest + sweeps + 1
    vmem = pl.BlockSpec(memory_space=pltpu.VMEM)
    smem = pl.BlockSpec(memory_space=pltpu.SMEM)
    dma = pltpu.SemaphoreType.DMA
    tall = width + width // 2
    return pl.pallas_call(
        functools.partial(kernel, rows_n, cols_n),
        out_shape=jax.ShapeDtypeStruct((height, columns), jnp.float32),
        in_specs=[smem, smem, vmem, vmem, vmem],
        out_specs=vmem,
        scratch_shapes=[
            pltpu.VMEM((widest, sweeps, 2, tall, span), jnp.float32),
            pltpu.VMEM((sweeps, tall, span), jnp.float32),
            pltpu.VMEM((widest, sweeps, 2 * span, 2 * span), jnp.bfloat16),
            pltpu.VMEM((widest, sweeps, 2 * span, 2 * span), jnp.bfloat16),
            pltpu.VMEM((slots, columns // 2, span), jnp.float32),
            pltpu.VMEM((per, columns, span), jnp.float32),
            pltpu.VMEM((per, columns, span), jnp.float32),
            dma((widest, sweeps)),
            dma((widest, sweeps)),
            dma((widest, sweeps)),
            dma((widest, sweeps)),
            dma((widest, sweeps)),
            dma((sweeps,)),
            dma((per, 2)),
            dma((slots,)),
            dma((sweeps,)),
            dma((sweeps,)),
            dma((widest,)),
            dma((per, 2)),
        ],
        compiler_params=pltpu.CompilerParams(collective_id=0, has_side_effects=True),
    )(order, offsets, eigvecs, jnp.swapaxes(reflectors, 2, 3), factors)


def solution(mesh):
    placed = (
        P("row", "col"),
        P(None, ("row", "col"), None, None),
        P(None, ("row", "col"), None, None),
        P(),
        P(),
    )
    body = functools.partial(local, mesh.shape["row"], mesh.shape["col"])
    return jax.shard_map(
        body, mesh=mesh, in_specs=placed, out_specs=P("row", "col"), check_vma=False
    )
```

time: 76 us -> 216 us (2.84)
  the two profiles are of different devices: /device:TPU:30 before, /device:TPU:18 now
where the time goes in v1:
time: 216 us; the launch traced here: 215 us
  Pallas kernels  214 us (99%)
    pallas_call x1, Pallas kernels, local(): pl.pallas_call(functools.partial(kernel, rows_n, cols_n), out_shape=jax.S...  214 us

profile of v1, /device:TPU:18, one launch (start us, length us, event | category | flops | bytes accessed | tf_op | source)
XLA Modules:
  0.0 215.5 jit_solution(8139838657809006134)
XLA Ops:
  0.0 213.9 %shard_map.55 = f32[256,128]{1,0:T(8,128)} custom-call(s32[8]{0:T(128)} %order_ref.1, s32[8]{0:T(128)} %off_ref.1, f32[256,128]{1,0:T(8,128)} %x_ref.1, f32[8,1,64,128]{3,2,1,0:T(8,128)} %bitcast.1, f32[8,1,64,64]{3,2,1,0:T(8,128)} %tri_ref.1), custom_call_target="tpu_custom_call" | custom-call | tf_op jit(solution)/shard_map/pallas_call | solution.py:460
  213.9 1.6 copy.7

commit v2 on v1

v2 whole, which is shorter than its diff:
```python
import functools

import jax
import jax.numpy as jnp
from jax import lax
from jax.experimental import pallas as pl
from jax.experimental.pallas import tpu as pltpu
from jax.sharding import PartitionSpec as P

MESH = pl.DeviceIdType.MESH
SKEW = 2
FORM_LEAD = 1
APPLY_LEAD = 5
CHUNK = 2


def split(x):
    hi = x.astype(jnp.bfloat16)
    lo = (x - hi.astype(jnp.float32)).astype(jnp.bfloat16)
    return hi, lo


def dot(a, b, dims=((1,), (0,))):
    return lax.dot_general(a, b, (dims, ((), ())), preferred_element_type=jnp.float32)


def product(a, b, dims=((1,), (0,))):
    (a_hi, a_lo), (b_hi, b_lo) = a, b
    return dot(a_hi, b_hi, dims) + (dot(a_hi, b_lo, dims) + dot(a_lo, b_hi, dims))


def shape_of_planes(rows_n, per, sweeps):
    planes = rows_n // 2
    own = 2 * per
    total = rows_n * per
    starts = [0] + [own * g + SKEW for g in range(1, planes)] + [total + sweeps - 1]
    most = count = 0
    for g in range(planes):
        begin, wide = starts[g], starts[g + 1] - starts[g]
        over = max(wide - 1 - (total - 1 - begin), 0)
        deep = min(sweeps, begin + wide) - 1
        count = max(count, (wide - 1) * sweeps + deep - over * (over + 1) // 2 + 1)
        for u in range(wide + sweeps - 1):
            live = [
                a for a in range(wide)
                if 0 <= u - a < sweeps and 0 <= begin + 2 * a - u < total
            ]
            most = max(most, len(live))
    widest = max(starts[g + 1] - starts[g] for g in range(planes))
    return planes, own, total, widest, most, count


def kernel(
    rows_n, cols_n, order_ref, off_ref, x_ref, house_ref, tri_ref, out_ref,
    pack, map_hi, map_lo, state, turned, final,
    arrive, beside, sent, send_z,
    tile_send, tile_recv, carry_send, carry_recv, last_send, last_recv, heard,
):
    row, col = lax.axis_index("row"), lax.axis_index("col")
    sweeps, _, width, span = house_ref.shape
    height, columns = x_ref.shape
    per = height // span
    half = columns // 2
    planes, own, total, widest, most, count = shape_of_planes(rows_n, per, sweeps)
    spare = state.shape[0] - 1
    plane, side = lax.div(row, 2), lax.rem(row, 2)
    pair, core = lax.div(col, 2), lax.rem(col, 2)
    row_x, col_y, col_b = row + 1 - 2 * side, lax.rem(col + cols_n // 2, cols_n), col + 1 - 2 * core
    top, bottom = plane == 0, plane == planes - 1

    def start_of(g):
        return jnp.where(g == 0, 0, own * g + SKEW)

    def end_of(g):
        return jnp.where(g == planes - 1, total + sweeps - 1, own * (g + 1) + SKEW)

    def plane_of(s):
        return jnp.minimum(lax.div(jnp.maximum(s - SKEW, 0), own), planes - 1)

    begin = start_of(plane)
    wide = end_of(plane) - begin
    steps = jnp.where(top, jnp.minimum(2 * wide - 1, wide + sweeps - 1), wide + sweeps - 1)

    def lowest(u):
        return jnp.maximum(
            jnp.maximum(u - (sweeps - 1), 0), lax.div(jnp.maximum(u - begin + 1, 0), 2)
        )

    def highest_of(u):
        return jnp.minimum(jnp.minimum(u, wide - 1), lax.div(total - 1 - begin + u, 2))

    def remote(src, dst, left, got, to_row, to_col):
        return pltpu.make_async_remote_copy(
            src_ref=src, dst_ref=dst, send_sem=left, recv_sem=got,
            device_id=(to_row, to_col), device_id_type=MESH,
        )

    barrier = pltpu.get_barrier_semaphore()
    nearest = ((row, col_b, True), (row_x, col, True), (row, col_y, True),
               (row - 2, col, jnp.logical_not(top)), (row + 2, col, jnp.logical_not(bottom)))

    def greet(flag):
        for to_row, to_col, valid in nearest:
            def one(to_row=to_row, to_col=to_col):
                pl.semaphore_signal(
                    flag, inc=1, device_id=(to_row, to_col), device_id_type=MESH
                )

            if valid is True:
                one()
            else:
                pl.when(valid)(one)

    greeted = 3 + jnp.where(top, 0, 1) + jnp.where(bottom, 0, 1)
    greet(barrier)

    mine = row * per + pair

    def place_of(a, p, first=begin):
        over = jnp.maximum(a - (total - 1 - first), 0)
        return a * sweeps + p - lax.div(over * (over + 1), 2)

    def goes_to(p):
        s = mine + p
        g = plane_of(s)
        return g, s - start_of(g)

    down = lax.broadcasted_iota(jnp.int32, (span, span), 0)
    across = lax.broadcasted_iota(jnp.int32, (span, span), 1)
    eye = jnp.where(down == across, 1.0, 0.0)

    def dense(p):
        stored = order_ref[p]
        house = pltpu.roll(house_ref[stored, 0], off_ref[stored] + width * core, 1)
        scaled = product(split(tri_ref[stored, 0].T), split(house))
        return eye - product(split(house.T), split(scaled))

    def stage(p):
        return count + p

    made = [dense(p) for p in range(sweeps)]
    for p in range(sweeps):
        g, a = goes_to(p)
        pack[jnp.where(g == plane, place_of(a, p), stage(p)), core] = made[p]

    def move(p, act, far):
        g, a = goes_to(p)
        apart = jnp.abs(g - plane)

        @pl.when((apart > 1) if far else (apart == 1))
        def _():
            there = place_of(a, p, start_of(g))
            act(remote(
                pack.at[stage(p), core], pack.at[there, core],
                send_z.at[p], arrive.at[there], 2 * g + side, col,
            ))

    def hand_out(t, h, act, keep):
        tile = row * per + t
        g = plane_of(jnp.maximum(tile - 1, 0))
        slot = tile - start_of(g) + sweeps - 1
        to_row = 2 * g + h

        @pl.when(to_row != row)
        def _():
            act(remote(
                turned.at[t, pl.ds(h * half, half)], state.at[slot],
                tile_send.at[t, h], tile_recv.at[slot], to_row, col,
            ))

        if keep:
            @pl.when(to_row == row)
            def _():
                state[slot] = turned[t, pl.ds(h * half, half), :]

    for t in range(per):
        turned[t] = x_ref[pl.ds(t * span, span), :].T

    @pl.when(bottom)
    def _():
        state[total - begin + sweeps - 1] = jnp.zeros((half, span), jnp.float32)

    pl.semaphore_wait(barrier, greeted)
    greet(heard)
    for p in range(sweeps):
        move(p, lambda c: c.start(), False)

    def reach():
        pl.semaphore_wait(heard, greeted)
        for t in range(per):
            for h in range(2):
                hand_out(t, h, lambda c: c.start(), True)
        for p in range(sweeps):
            move(p, lambda c: c.start(), True)

    def route(a, p):
        j = begin + a - p
        home_row = lax.div(j, per)
        same_x = side == lax.rem(home_row, 2)
        same_y = pair == lax.rem(j, per)
        native = lax.div(home_row, 2) == plane
        by_x = lax.rem(p, 2) == 0
        return same_x, same_y, native, by_x

    def copies(a, p):
        n = place_of(a, p)
        place = pack.at[n, core]
        return (
            remote(place, place, sent.at[n], arrive.at[n], row_x, col),
            remote(place, place, sent.at[n], arrive.at[n], row, col_y),
            remote(place, place, sent.at[n], beside.at[n], row, col_b),
        )

    def each(u, act):
        low, high = lowest(u), highest_of(u)

        def one(a, _):
            act(a, u - a)
            return 0

        lax.fori_loop(low, high + 1, one, 0)

    def spread(own_source):
        def one(a, p):
            same_x, same_y, native, _ = route(a, p)
            chosen = native if own_source else jnp.logical_not(native)

            @pl.when(same_x & same_y & chosen)
            def _():
                by_x, by_y, by_b = copies(a, p)
                if not own_source:
                    by_x.wait_recv()
                by_x.start()
                by_y.start()
                by_b.start()

        return one

    def relay(a, p):
        same_x, same_y, _, first_x = route(a, p)

        @pl.when(same_x != same_y)
        def _():
            by_x, by_y, by_b = copies(a, p)
            by_x.wait_recv()

            @pl.when(same_x & jnp.logical_not(first_x))
            def _():
                by_x.start()

            @pl.when(same_y & first_x)
            def _():
                by_y.start()

            by_b.start()

    def finish_ring(a, p):
        same_x, same_y, _, _ = route(a, p)

        @pl.when(jnp.logical_not(same_x | same_y))
        def _():
            by_x, _, by_b = copies(a, p)
            by_x.wait_recv()
            by_b.start()

    def settle(a, p):
        same_x, same_y, _, first_x = route(a, p)
        onward = (same_x & jnp.logical_not(first_x)) | (same_y & first_x)
        times = 1 + jnp.where(same_x & same_y, 2, jnp.where(onward, 1, 0))
        n = place_of(a, p)
        for k in range(1, 4):
            @pl.when(times == k)
            def _(k=k):
                whole = pack.at[pl.ds(0, k), core]
                remote(whole, whole, sent.at[n], arrive.at[n], row_x, col).wait_send()

    def others(a, p):
        n = place_of(a, p)
        place = pack.at[n, 1 - core]
        remote(place, place, sent.at[n], beside.at[n], row, col_b).wait_recv()

    def compose(a, p):
        offset = off_ref[order_ref[p]]
        first, second = pack[place_of(a, p), 0], pack[place_of(a, p), 1]
        zero = jnp.zeros_like(eye)
        row_0, row_1 = down >= offset, down >= offset + width
        col_0, col_1 = across >= offset, across >= offset + width
        middle = ((across - offset) & (span - 1)) >= width
        both = product(split(jnp.where(middle, first, 0.0)), split(second))
        ahead = jnp.where(col_1, both, first)
        quarters = (
            jnp.where(row_0 & col_0, ahead, eye),
            jnp.where(row_0 & jnp.logical_not(col_1), both, zero),
            jnp.where(
                row_0,
                jnp.where(jnp.logical_not(row_1) & col_1, second, zero),
                jnp.where(col_0, ahead, zero),
            ),
            jnp.where(
                row_1 | col_1, eye, jnp.where(row_0, second, both)
            ),
        )
        return [split(q) for q in quarters]

    def form(u):
        low, high = lowest(u), highest_of(u)

        def some(q, _):
            spots = [jnp.minimum(low + q * CHUNK + i, high) for i in range(CHUNK)]
            made = [compose(a, u - a) for a in spots]
            for a, quarters in zip(spots, made):
                for n, (hi, lo) in enumerate(quarters):
                    part = pl.ds(n // 2 * span, span), pl.ds(n % 2 * span, span)
                    map_hi[place_of(a, u - a), *part] = hi
                    map_lo[place_of(a, u - a), *part] = lo
            return 0

        lax.fori_loop(0, lax.div(high - low + CHUNK, CHUNK), some, 0)

    def carry(p, slot):
        return remote(
            state.at[slot], state.at[sweeps - 1 - p], carry_send.at[p], carry_recv.at[p],
            row + 2, col,
        )

    def finish(a, act, keep):
        j = begin + a - (sweeps - 1)
        to_row = lax.div(j, per)
        t = lax.rem(j, per)
        place = pl.ds(side * half, half)

        @pl.when(to_row != row)
        def _():
            act(remote(
                state.at[a], final.at[t, place], last_send.at[a], last_recv.at[t, side],
                to_row, col,
            ))

        if keep:
            @pl.when(to_row == row)
            def _():
                final[t, place, :] = state[a]

    def lasts(u):
        a = u - (sweeps - 1)
        return (a >= 0) & (a == lowest(u)) & (a <= highest_of(u))

    def passes(u):
        return (highest_of(u) == wide - 1) & (lowest(u) <= wide - 1) & jnp.logical_not(bottom)

    def spills(u):
        p = u - wide + 1
        return passes(u) & (begin + wide - 1 - p == 0) & (p < sweeps - 1)

    def apply(u):
        low, high = lowest(u), highest_of(u)
        tile = begin + u + 1

        @pl.when((u < wide) & (tile < total) & (lax.div(tile, per) != row))
        def _():
            remote(
                state.at[u + sweeps], state.at[u + sweeps], tile_send.at[0, 0],
                tile_recv.at[u + sweeps], row_x, col,
            ).wait_recv()

        @pl.when(top & (u == 0) & (row != 0))
        def _():
            remote(
                state.at[sweeps - 1], state.at[sweeps - 1], tile_send.at[0, 0],
                tile_recv.at[sweeps - 1], row_x, col,
            ).wait_recv()

        @pl.when((low == 0) & jnp.logical_not(top))
        def _():
            carry(u, sweeps - 1 - u).wait_recv()

        def some(live):
            ready = []
            for i in range(live):
                a = low + i
                p = u - a
                x = jnp.concatenate([state[a - p + sweeps - 1], state[a - p + sweeps]], 1)
                n = place_of(a, p)
                ready.append((a, p, x, map_hi[n], map_lo[n]))
            made = []
            for a, p, x, hi, lo in ready:
                x_hi, x_lo = split(x)
                both = dot(jnp.concatenate([x_hi, x_lo], 0), hi)
                made.append((a, p, both[:half] + (both[half:] + dot(x_hi, lo))))
            for a, p, y in made:
                state[a - p + sweeps - 1] = y[:, :span]
                to = jnp.where(begin + a - p == total - 1, spare, a - p + sweeps)
                state[to] = y[:, span:]

        for live in range(1, most + 1):
            @pl.when(high - low + 1 == live)
            def _(live=live):
                some(live)

        @pl.when(passes(u))
        def _():
            p = u - wide + 1
            carry(p, wide - 1 - p + sweeps).start()

        @pl.when(spills(u))
        def _():
            p = u - wide + 1
            carry(p + 1, wide - 1 - p + sweeps - 1).start()

        @pl.when(lasts(u))
        def _():
            finish(u - (sweeps - 1), lambda c: c.start(), True)

    def run(*acts):
        def one(v, _):
            for act in acts:
                each(v, act)
            return 0

        lax.fori_loop(0, steps, one, 0)

    run(spread(True))
    reach()
    run(spread(False))
    run(relay)
    lead = jnp.minimum(FORM_LEAD + APPLY_LEAD * plane, FORM_LEAD + steps)

    def main(v, _):
        @pl.when(v < steps)
        def _():
            each(v, finish_ring)

        w = v - FORM_LEAD

        @pl.when((w >= 0) & (w < steps))
        def _():
            each(w, others)
            form(w)

        u = v - lead

        @pl.when(u >= 0)
        def _():
            apply(u)

        return 0

    lax.fori_loop(0, steps + lead, main, 0)

    def drain(u, _):
        each(u, settle)

        @pl.when(passes(u))
        def _():
            p = u - wide + 1
            carry(p, wide - 1 - p + sweeps).wait_send()

        @pl.when(spills(u))
        def _():
            p = u - wide + 1
            carry(p + 1, wide - 1 - p + sweeps - 1).wait_send()

        @pl.when(lasts(u))
        def _():
            finish(u - (sweeps - 1), lambda c: c.wait_send(), False)

        return 0

    lax.fori_loop(0, steps, drain, 0)
    for p in range(sweeps):
        move(p, lambda c: c.wait_send(), False)
        move(p, lambda c: c.wait_send(), True)
    for t in range(per):
        for h in range(2):
            hand_out(t, h, lambda c: c.wait_send(), False)
    for t in range(per):
        g = plane_of(row * per + t + sweeps - 1)
        for h in range(2):
            @pl.when(2 * g + h != row)
            def _(t=t, h=h):
                place = final.at[t, pl.ds(h * half, half)]
                remote(
                    place, place, last_send.at[0], last_recv.at[t, h], row_x, col
                ).wait_recv()

        out_ref[pl.ds(t * span, span), :] = final[t].T


def local(rows_n, cols_n, eigvecs, reflectors, factors, order, offsets):
    sweeps, _, span, width = reflectors.shape
    height, columns = eigvecs.shape
    per = height // span
    _, _, _, widest, _, count = shape_of_planes(rows_n, per, sweeps)
    slots = widest + sweeps + 1
    vmem = pl.BlockSpec(memory_space=pltpu.VMEM)
    smem = pl.BlockSpec(memory_space=pltpu.SMEM)
    dma = pltpu.SemaphoreType.DMA
    return pl.pallas_call(
        functools.partial(kernel, rows_n, cols_n),
        out_shape=jax.ShapeDtypeStruct((height, columns), jnp.float32),
        in_specs=[smem, smem, vmem, vmem, vmem],
        out_specs=vmem,
        scratch_shapes=[
            pltpu.VMEM((count + sweeps, 2, span, span), jnp.float32),
            pltpu.VMEM((count, 2 * span, 2 * span), jnp.bfloat16),
            pltpu.VMEM((count, 2 * span, 2 * span), jnp.bfloat16),
            pltpu.VMEM((slots, columns // 2, span), jnp.float32),
            pltpu.VMEM((per, columns, span), jnp.float32),
            pltpu.VMEM((per, columns, span), jnp.float32),
            dma((count,)),
            dma((count,)),
            dma((count,)),
            dma((sweeps,)),
            dma((per, 2)),
            dma((slots,)),
            dma((sweeps,)),
            dma((sweeps,)),
            dma((widest,)),
            dma((per, 2)),
            pltpu.SemaphoreType.REGULAR,
        ],
        compiler_params=pltpu.CompilerParams(collective_id=0, has_side_effects=True),
    )(order, offsets, eigvecs, jnp.swapaxes(reflectors, 2, 3), factors)


def solution(mesh):
    placed = (
        P("row", "col"),
        P(None, ("row", "col"), None, None),
        P(None, ("row", "col"), None, None),
        P(),
        P(),
    )
    body = functools.partial(local, mesh.shape["row"], mesh.shape["col"])
    return jax.shard_map(
        body, mesh=mesh, in_specs=placed, out_specs=P("row", "col"), check_vma=False
    )
```

time: 216 us -> 53.8 us (0.25)
  Pallas kernels: 214 us -> 51.7 us
    pallas_call x1, Pallas kernels: 214 us -> 51.7 us  [local(): pl.pallas_call(functools.partial(kernel, rows_n, cols_n), out_shape=jax.S...]
where the time goes in v2:
time: 53.8 us; the launch traced here: 53.3 us
  Pallas kernels  51.7 us (96%)
  local copies, waits for them, and re-layouts  1.57 us (3%)
    pallas_call x1, Pallas kernels, local(): pl.pallas_call(functools.partial(kernel, rows_n, cols_n), out_shape=jax.S...  51.7 us
    unnamed x1, local copies, waits for them, and re-layouts  1.57 us

profile of v2, /device:TPU:18, one launch (start us, length us, event | category | flops | bytes accessed | tf_op | source)
XLA Modules:
  0.0 53.3 jit_solution(13137954190924378567)
XLA Ops:
  0.0 51.7 %shard_map.55 = f32[256,128]{1,0:T(8,128)} custom-call(s32[8]{0:T(128)} %order_ref.1, s32[8]{0:T(128)} %off_ref.1, f32[256,128]{1,0:T(8,128)} %x_ref.1, f32[8,1,64,128]{3,2,1,0:T(8,128)} %bitcast.1, f32[8,1,64,64]{3,2,1,0:T(8,128)} %tri_ref.1), custom_call_target="tpu_custom_call" | custom-call | tf_op jit(solution)/shard_map/pallas_call | solution.py:498
  51.8 1.6 %copy.7 = f32[256,128]{1,0:T(8,128)} copy(f32[256,128]{1,0:T(8,128)} %shard_map.55) | data formatting | bytes 262144

commit v3 on v2

v3 whole, which is shorter than its diff:
```python
import functools

import jax
import jax.numpy as jnp
from jax import lax
from jax.experimental import pallas as pl
from jax.experimental.pallas import tpu as pltpu
from jax.sharding import PartitionSpec as P

MESH = pl.DeviceIdType.MESH
SKEWS = (0, 1, 2, 3)
APPLY_LEAD = 1
FORM_LAG = 1
STRIP = 32
STRIDE = 2
EARLY = 4


def split(x):
    hi = x.astype(jnp.bfloat16)
    lo = (x - hi.astype(jnp.float32)).astype(jnp.bfloat16)
    return hi, lo


def dot(a, b, dims=((1,), (0,))):
    return lax.dot_general(a, b, (dims, ((), ())), preferred_element_type=jnp.float32)


def product(a, b, dims=((1,), (0,))):
    (a_hi, a_lo), (b_hi, b_lo) = a, b
    return dot(a_hi, b_hi, dims) + (dot(a_hi, b_lo, dims) + dot(a_lo, b_hi, dims))


def shape_of_planes(rows_n, per, sweeps):
    planes = rows_n // 2
    own = 2 * per
    total = rows_n * per
    starts = [0] + [own * g + SKEWS[min(g, len(SKEWS) - 1)] for g in range(1, planes)] + [total + sweeps - 1]
    most = count = 0
    for g in range(planes):
        begin, wide = starts[g], starts[g + 1] - starts[g]
        over = max(wide - 1 - (total - 1 - begin), 0)
        deep = min(sweeps, begin + wide) - 1
        count = max(count, (wide - 1) * sweeps + deep - over * (over + 1) // 2 + 1)
        for u in range(wide + STRIDE * (sweeps - 1)):
            live = [
                p for p in range(sweeps)
                if 0 <= u - STRIDE * p < wide
                and 0 <= begin + u - (STRIDE + 1) * p < total
            ]
            most = max(most, len(live))
    widest = max(starts[g + 1] - starts[g] for g in range(planes))
    return planes, own, total, widest, most, count


def kernel(
    rows_n, cols_n, order_ref, off_ref, x_ref, house_ref, tri_ref, out_ref,
    pack, map_hi, map_lo, state, turned, final,
    arrive, beside, sent, send_z,
    tile_send, tile_recv, carry_send, carry_recv, last_send, last_recv, heard,
):
    row, col = lax.axis_index("row"), lax.axis_index("col")
    sweeps, _, width, span = house_ref.shape
    height, columns = x_ref.shape
    per = height // span
    half = columns // 2
    planes, own, total, widest, most, count = shape_of_planes(rows_n, per, sweeps)
    spare = state.shape[0] - 1
    plane, side = lax.div(row, 2), lax.rem(row, 2)
    pair, core = lax.div(col, 2), lax.rem(col, 2)
    row_x, col_y, col_b = row + 1 - 2 * side, lax.rem(col + cols_n // 2, cols_n), col + 1 - 2 * core
    top, bottom = plane == 0, plane == planes - 1

    def start_of(g):
        skew = SKEWS[-1]
        for n in range(len(SKEWS) - 2, -1, -1):
            skew = jnp.where(g == n, SKEWS[n], skew)
        return own * g + skew

    def end_of(g):
        return jnp.where(g == planes - 1, total + sweeps - 1, start_of(g + 1))

    def plane_of(s):
        g = jnp.minimum(lax.div(s, own), planes - 1)
        return g - jnp.where(s < start_of(g), 1, 0)

    begin = start_of(plane)
    wide = end_of(plane) - begin
    deepest = jnp.where(top, jnp.minimum(sweeps - 1, wide - 1), sweeps - 1)
    steps = wide + STRIDE * deepest

    def window(u):
        def over(x, n):
            return lax.div(jnp.maximum(x, 0) + n - 1, n)

        low = jnp.maximum(over(u - wide + 1, STRIDE), over(begin + u - total + 1, STRIDE + 1))
        high = jnp.minimum(lax.div(u, STRIDE), lax.div(begin + u, STRIDE + 1))
        return low, jnp.minimum(high, sweeps - 1)

    def remote(src, dst, left, got, to_row, to_col):
        return pltpu.make_async_remote_copy(
            src_ref=src, dst_ref=dst, send_sem=left, recv_sem=got,
            device_id=(to_row, to_col), device_id_type=MESH,
        )

    barrier = pltpu.get_barrier_semaphore()
    nearest = ((row, col_b, True), (row_x, col, True), (row, col_y, True),
               (row - 2, col, jnp.logical_not(top)), (row + 2, col, jnp.logical_not(bottom)))

    def greet(flag):
        for to_row, to_col, valid in nearest:
            def one(to_row=to_row, to_col=to_col):
                pl.semaphore_signal(
                    flag, inc=1, device_id=(to_row, to_col), device_id_type=MESH
                )

            if valid is True:
                one()
            else:
                pl.when(valid)(one)

    greeted = 3 + jnp.where(top, 0, 1) + jnp.where(bottom, 0, 1)
    greet(barrier)

    mine = row * per + pair

    def place_of(a, p, first=begin):
        over = jnp.maximum(a - (total - 1 - first), 0)
        return a * sweeps + p - lax.div(over * (over + 1), 2)

    def goes_to(p):
        s = mine + p
        g = plane_of(s)
        return g, s - start_of(g)

    down = lax.broadcasted_iota(jnp.int32, (span, span), 0)
    across = lax.broadcasted_iota(jnp.int32, (span, span), 1)
    eye = jnp.where(down == across, 1.0, 0.0)

    def dense(p):
        stored = order_ref[p]
        house = pltpu.roll(house_ref[stored, 0], off_ref[stored] + width * core, 1)
        scaled = product(split(tri_ref[stored, 0].T), split(house))
        return eye - product(split(house.T), split(scaled))

    def stage(p):
        return count + p

    def prepare(low, high):
        made = [dense(p) for p in range(low, high)]
        for p in range(low, high):
            g, a = goes_to(p)
            pack[jnp.where(g == plane, place_of(a, p), stage(p)), core] = made[p - low]

    def move(p, act, far):
        g, a = goes_to(p)
        apart = jnp.abs(g - plane)

        @pl.when((apart > 1) if far else (apart == 1))
        def _():
            there = place_of(a, p, start_of(g))
            act(remote(
                pack.at[stage(p), core], pack.at[there, core],
                send_z.at[p], arrive.at[there], 2 * g + side, col,
            ))

    def hand_out(t, h, act, keep):
        tile = row * per + t
        g = plane_of(jnp.maximum(tile - 1, 0))
        slot = tile - start_of(g) + sweeps - 1
        to_row = 2 * g + h

        @pl.when(to_row != row)
        def _():
            act(remote(
                turned.at[t, pl.ds(h * half, half)], state.at[slot],
                tile_send.at[t, h], tile_recv.at[slot], to_row, col,
            ))

        if keep:
            @pl.when(to_row == row)
            def _():
                state[slot] = turned[t, pl.ds(h * half, half), :]

    def reach():
        pl.semaphore_wait(heard, greeted)
        for p in range(sweeps):
            move(p, lambda c: c.start(), True)

    kin = per
    most_lines = -(-widest // own)
    here = side * kin + pair
    over_x, over_y = (1 - side) * kin + pair, side * kin + (kin - 1 - pair)
    over_both = (1 - side) * kin + (kin - 1 - pair)

    def copies(a, p):
        n = place_of(a, p)
        place = pack.at[n, core]
        return (
            remote(place, place, sent.at[p], arrive.at[n], row_x, col),
            remote(place, place, sent.at[p], arrive.at[n], row, col_y),
            remote(place, place, sent.at[p], beside.at[n], row, col_b),
            remote(place, place, sent.at[p], arrive.at[n], row_x, col_y),
        )

    def line(which, p):
        low = jnp.maximum(begin - p, 0)
        high = jnp.minimum(begin + wide - 1 - p, total - 1)
        low = low + lax.rem(which - lax.rem(low, own) + own, own)
        return low, lax.div(jnp.maximum(high - low + own, 0), own)

    def kind(which, p, act, skip=0):
        low, many = line(which, p)

        def one(i, _):
            j = low + i * own
            act(j - begin + p, p, j)
            return 0

        lax.fori_loop(skip, many, one, 0)

    def is_native(j):
        return lax.div(j, own) == plane

    def sow(a, p, j):
        native = is_native(j)
        by_x, by_y, by_b, by_both = copies(a, p)

        @pl.when(jnp.logical_not(native))
        def _():
            by_x.wait_recv()

        by_x.start()
        by_y.start()

        @pl.when(direct(j))
        def _():
            by_both.start()

        by_b.start()

    def direct(j):
        return top & jnp.logical_not(is_native(j))

    def only(test, wanted, act):
        def one(a, p, j):
            @pl.when(test(j) if wanted else jnp.logical_not(test(j)))
            def _():
                act(a, p, j)

        return one

    def onward_x(p):
        return lax.rem(p, 2) == 1

    def relay_x(a, p, j):
        by_x, by_y, by_b, _ = copies(a, p)
        by_x.wait_recv()

        @pl.when(jnp.logical_not(onward_x(p) | direct(j)))
        def _():
            by_y.start()

        by_b.start()

    def relay_y(a, p, j):
        by_x, by_y, by_b, _ = copies(a, p)
        by_x.wait_recv()

        @pl.when(onward_x(p) & jnp.logical_not(direct(j)))
        def _():
            by_x.start()

        by_b.start()

    def close(a, p, j):
        by_x, _, by_b, _ = copies(a, p)
        by_x.wait_recv()
        by_b.start()

    def form(*spots):
        places = [(place_of(a, p), p) for a, p in spots]
        for n, _ in places:
            beyond = pack.at[n, 1 - core]
            remote(beyond, beyond, sent.at[0], beside.at[n], row, col_b).wait_recv()
        joint = []
        for n, p in places:
            offset = off_ref[order_ref[p]]
            middle = ((across - offset) & (span - 1)) >= width
            joint.append(
                product(split(jnp.where(middle, pack[n, 0], 0.0)), split(pack[n, 1]))
            )
        for (n, p), joined in zip(places, joint):
            offset = off_ref[order_ref[p]]
            for r in range(0, span, STRIP):
                rows = pl.ds(r, STRIP)
                down_r = r + lax.broadcasted_iota(jnp.int32, (STRIP, span), 0)
                across_r = lax.broadcasted_iota(jnp.int32, (STRIP, span), 1)
                unit = jnp.where(down_r == across_r, 1.0, 0.0)
                row_0, row_1 = down_r >= offset, down_r >= offset + width
                col_0, col_1 = across_r >= offset, across_r >= offset + width
                first, second = pack[n, 0, rows, :], pack[n, 1, rows, :]
                both = joined[r : r + STRIP]
                ahead = jnp.where(col_1, both, first)
                quarters = (
                    jnp.where(row_0 & col_0, ahead, unit),
                    jnp.where(row_0 & jnp.logical_not(col_1), both, 0.0),
                    jnp.where(
                        row_0,
                        jnp.where(jnp.logical_not(row_1) & col_1, second, 0.0),
                        jnp.where(col_0, ahead, 0.0),
                    ),
                    jnp.where(row_1 | col_1, unit, jnp.where(row_0, second, both)),
                )
                for q, quarter in enumerate(quarters):
                    hi, lo = split(quarter)
                    part = pl.ds(q // 2 * span + r, STRIP), pl.ds(q % 2 * span, span)
                    map_hi[n, *part] = hi
                    map_lo[n, *part] = lo

    def form_one(a, p, j):
        form((a, p))

    def form_near(p):
        lines = [line(which, p) for which in (here, over_x, over_y)]
        full = True
        for low, many in lines:
            full = full & (many > 0) & jnp.logical_not(direct(low))

        @pl.when(full)
        def _():
            form(*[(low - begin + p, p) for low, _ in lines])

        skip = jnp.where(full, 1, 0)
        for which in (here, over_x, over_y):
            kind(which, p, only(direct, False, form_one), skip)

    def carry(p, slot):
        return remote(
            state.at[slot], state.at[sweeps - 1 - p], carry_send.at[p], carry_recv.at[p],
            row + 2, col,
        )

    def finish(a, act, keep):
        j = begin + a - (sweeps - 1)
        to_row = lax.div(j, per)
        t = lax.rem(j, per)
        place = pl.ds(side * half, half)

        @pl.when(to_row != row)
        def _():
            act(remote(
                state.at[a], final.at[t, place], last_send.at[a], last_recv.at[t, side],
                to_row, col,
            ))

        if keep:
            @pl.when(to_row == row)
            def _():
                final[t, place, :] = state[a]

    def lasts(u):
        low, high = window(u)
        return (high == sweeps - 1) & (low <= high)

    def passes(u):
        low, high = window(u)
        return (u - STRIDE * low == wide - 1) & (low <= high) & jnp.logical_not(bottom)

    def spills(u):
        p = window(u)[0]
        return passes(u) & (begin + wide - 1 - p == 0) & (p < sweeps - 1)

    def apply(u):
        low, high = window(u)
        tile = begin + u + 1

        @pl.when((u < wide) & (tile < total) & (lax.div(tile, per) != row))
        def _():
            remote(
                state.at[u + sweeps], state.at[u + sweeps], tile_send.at[0, 0],
                tile_recv.at[u + sweeps], row_x, col,
            ).wait_recv()

        @pl.when(top & (u == 0) & (row != 0))
        def _():
            remote(
                state.at[sweeps - 1], state.at[sweeps - 1], tile_send.at[0, 0],
                tile_recv.at[sweeps - 1], row_x, col,
            ).wait_recv()

        @pl.when((u == STRIDE * high) & (low <= high) & jnp.logical_not(top))
        def _():
            carry(high, sweeps - 1 - high).wait_recv()

        def some(live):
            ready = []
            for i in range(live):
                p = low + i
                a = u - STRIDE * p
                x = jnp.concatenate([state[a - p + sweeps - 1], state[a - p + sweeps]], 1)
                n = place_of(a, p)
                ready.append((a, p, x, map_hi[n], map_lo[n]))
            made = []
            for a, p, x, hi, lo in ready:
                x_hi, x_lo = split(x)
                both = dot(jnp.concatenate([x_hi, x_lo], 0), hi)
                made.append((a, p, both[:half] + (both[half:] + dot(x_hi, lo))))
            for a, p, y in made:
                state[a - p + sweeps - 1] = y[:, :span]
                to = jnp.where(begin + a - p == total - 1, spare, a - p + sweeps)
                state[to] = y[:, span:]

        for live in range(1, most + 1):
            @pl.when(high - low + 1 == live)
            def _(live=live):
                some(live)

        @pl.when(passes(u))
        def _():
            p = window(u)[0]
            carry(p, wide - 1 - p + sweeps).start()

        @pl.when(spills(u))
        def _():
            p = window(u)[0]
            carry(p + 1, wide - 1 - p + sweeps - 1).start()

        @pl.when(lasts(u))
        def _():
            finish(u - STRIDE * (sweeps - 1), lambda c: c.start(), True)

    def over_sweeps(act):
        def one(p, _):
            act(p)
            return 0

        lax.fori_loop(0, sweeps, one, 0)

    def turn(v):
        return v

    def near(v, _):
        @pl.when(v < sweeps)
        def _():
            kind(over_x, turn(v), only(direct, False, relay_x))
            kind(over_y, turn(v), only(direct, False, relay_y))

        p = v - FORM_LAG

        @pl.when(p >= 0)
        def _():
            form_near(turn(p))

        return 0

    def drain_maps(p):
        lines = [line(which, p)[1] for which in (here, over_x, over_y, over_both)]
        straight = [jnp.where(top, jnp.maximum(many - 1, 0), 0) for many in lines]
        turns = jnp.where(onward_x(p), 1, 0)
        total_sends = (
            3 * lines[0] + straight[0] + lines[3]
            + lines[1] + (1 - turns) * (lines[1] - straight[1])
            + lines[2] + turns * (lines[2] - straight[2])
        )
        for k in range(1, 3 * most_lines + 5 * most_lines + 1):
            @pl.when(total_sends == k)
            def _(k=k):
                whole = pack.at[pl.ds(0, k), core]
                remote(whole, whole, sent.at[p], arrive.at[0], row_x, col).wait_send()

    def main(v, _):
        @pl.when(v < sweeps)
        def _():
            kind(over_both, v, close)

            @pl.when(top)
            def _():
                kind(over_x, v, only(direct, True, close))
                kind(over_y, v, only(direct, True, close))

        p = v - FORM_LAG

        @pl.when((p >= 0) & (p < sweeps))
        def _():
            kind(over_both, p, form_one)

            @pl.when(top)
            def _():
                for which in (here, over_x, over_y):
                    kind(which, p, only(direct, True, form_one))

        @pl.when((v == sweeps + FORM_LAG) & (plane > 1))
        def _():
            over_sweeps(drain_maps)

        def one(k, _):
            u = (v - lead) * STRIDE + k

            @pl.when((u >= 0) & (u < steps))
            def _():
                apply(u)

            return 0

        lax.fori_loop(0, STRIDE, one, 0)
        return 0

    def begin_sweeps(low, high):
        for p in range(low, high):
            move(p, lambda c: c.start(), False)

        def one(p, _):
            kind(here, p, only(is_native, True, sow))
            return 0

        lax.fori_loop(low, high, one, 0)

    prepare(0, EARLY)
    pl.semaphore_wait(barrier, greeted)
    greet(heard)
    begin_sweeps(0, EARLY)
    prepare(EARLY, sweeps)
    begin_sweeps(EARLY, sweeps)
    for t in range(per):
        turned[t] = x_ref[pl.ds(t * span, span), :].T

    @pl.when(bottom)
    def _():
        state[total - begin + sweeps - 1] = jnp.zeros((half, span), jnp.float32)


    reach()
    over_sweeps(lambda p: kind(here, p, only(is_native, False, sow)))
    for t in range(per):
        for h in range(2):
            hand_out(t, h, lambda c: c.start(), True)
    lax.fori_loop(0, sweeps + FORM_LAG, near, 0)
    lead = FORM_LAG + jnp.where(top, 0, jnp.where(plane == 1, APPLY_LEAD, sweeps))
    lax.fori_loop(
        0, jnp.maximum(sweeps + FORM_LAG + 1, lax.div(steps + STRIDE - 1, STRIDE) + lead), main, 0
    )

    def drain(u, _):

        @pl.when(passes(u))
        def _():
            p = window(u)[0]
            carry(p, wide - 1 - p + sweeps).wait_send()

        @pl.when(spills(u))
        def _():
            p = window(u)[0]
            carry(p + 1, wide - 1 - p + sweeps - 1).wait_send()

        @pl.when(lasts(u))
        def _():
            finish(u - STRIDE * (sweeps - 1), lambda c: c.wait_send(), False)

        return 0

    lax.fori_loop(0, steps, drain, 0)

    @pl.when(plane <= 1)
    def _():
        over_sweeps(drain_maps)

    for p in range(sweeps):
        move(p, lambda c: c.wait_send(), False)
        move(p, lambda c: c.wait_send(), True)
    for t in range(per):
        for h in range(2):
            hand_out(t, h, lambda c: c.wait_send(), False)
    for t in range(per):
        g = plane_of(row * per + t + sweeps - 1)
        for h in range(2):
            @pl.when(2 * g + h != row)
            def _(t=t, h=h):
                place = final.at[t, pl.ds(h * half, half)]
                remote(
                    place, place, last_send.at[0], last_recv.at[t, h], row_x, col
                ).wait_recv()

        out_ref[pl.ds(t * span, span), :] = final[t].T


def local(rows_n, cols_n, eigvecs, reflectors, factors, order, offsets):
    sweeps, _, span, width = reflectors.shape
    height, columns = eigvecs.shape
    per = height // span
    _, _, _, widest, _, count = shape_of_planes(rows_n, per, sweeps)
    slots = widest + sweeps + 1
    vmem = pl.BlockSpec(memory_space=pltpu.VMEM)
    smem = pl.BlockSpec(memory_space=pltpu.SMEM)
    dma = pltpu.SemaphoreType.DMA
    return pl.pallas_call(
        functools.partial(kernel, rows_n, cols_n),
        out_shape=jax.ShapeDtypeStruct((height, columns), jnp.float32),
        in_specs=[smem, smem, vmem, vmem, vmem],
        out_specs=vmem,
        scratch_shapes=[
            pltpu.VMEM((count + sweeps, 2, span, span), jnp.float32),
            pltpu.VMEM((count, 2 * span, 2 * span), jnp.bfloat16),
            pltpu.VMEM((count, 2 * span, 2 * span), jnp.bfloat16),
            pltpu.VMEM((slots, columns // 2, span), jnp.float32),
            pltpu.VMEM((per, columns, span), jnp.float32),
            pltpu.VMEM((per, columns, span), jnp.float32),
            dma((count,)),
            dma((count,)),
            dma((sweeps,)),
            dma((sweeps,)),
            dma((per, 2)),
            dma((slots,)),
            dma((sweeps,)),
            dma((sweeps,)),
            dma((widest,)),
            dma((per, 2)),
            pltpu.SemaphoreType.REGULAR,
        ],
        compiler_params=pltpu.CompilerParams(collective_id=0, has_side_effects=True),
    )(order, offsets, eigvecs, jnp.swapaxes(reflectors, 2, 3), factors)


def solution(mesh):
    placed = (
        P("row", "col"),
        P(None, ("row", "col"), None, None),
        P(None, ("row", "col"), None, None),
        P(),
        P(),
    )
    body = functools.partial(local, mesh.shape["row"], mesh.shape["col"])
    return jax.shard_map(
        body, mesh=mesh, in_specs=placed, out_specs=P("row", "col"), check_vma=False
    )
```

time: 53.8 us -> 48.8 us (0.907)
  Pallas kernels: 51.7 us -> 47.1 us
    pallas_call x1, Pallas kernels: 51.7 us -> 47.1 us  [local(): pl.pallas_call(functools.partial(kernel, rows_n, cols_n), out_shape=jax.S...]
where the time goes in v3:
time: 48.8 us; the launch traced here: 48.6 us
  Pallas kernels  47.1 us (97%)
  local copies, waits for them, and re-layouts  1.57 us (3%)
    pallas_call x1, Pallas kernels, local(): pl.pallas_call(functools.partial(kernel, rows_n, cols_n), out_shape=jax.S...  47.1 us
    unnamed x1, local copies, waits for them, and re-layouts  1.57 us

profile of v3, /device:TPU:18, one launch (start us, length us, event | category | flops | bytes accessed | tf_op | source)
XLA Modules:
  0.0 48.6 jit_solution(1089651537565008623)
XLA Ops:
  0.0 47.1 %shard_map.55 = f32[256,128]{1,0:T(8,128)} custom-call(s32[8]{0:T(128)} %order_ref.1, s32[8]{0:T(128)} %off_ref.1, f32[256,128]{1,0:T(8,128)} %x_ref.1, f32[8,1,64,128]{3,2,1,0:T(8,128)} %bitcast.1, f32[8,1,64,64]{3,2,1,0:T(8,128)} %tri_ref.1), custom_call_target="tpu_custom_call" | custom-call | tf_op jit(solution)/shard_map/pallas_call | solution.py:596
  47.1 1.6 %copy.7 = f32[256,128]{1,0:T(8,128)} copy(f32[256,128]{1,0:T(8,128)} %shard_map.55) | data formatting | bytes 262144

commit v4 on v3

--- a/solution.py
+++ b/solution.py
@@ -13,7 +13,7 @@
 FORM_LAG = 1
 STRIP = 32
 STRIDE = 2
-EARLY = 4
+EARLY = 2
 
 
 def split(x):
@@ -54,7 +54,8 @@
 
 
 def kernel(
-    rows_n, cols_n, order_ref, off_ref, x_ref, house_ref, tri_ref, out_ref,
+    rows_n, cols_n, order_ref, off_ref, x_hbm, house_hbm, tri_hbm, out_ref,
+    x_ref, house_ref, tri_ref, load_sem,
     pack, map_hi, map_lo, state, turned, final,
     arrive, beside, sent, send_z,
     tile_send, tile_recv, carry_send, carry_recv, last_send, last_recv, heard,
@@ -103,6 +104,14 @@
             device_id=(to_row, to_col), device_id_type=MESH,
         )
 
+    loads = [
+        pltpu.make_async_copy(src, dst, load_sem.at[n])
+        for n, (src, dst) in enumerate(
+            ((house_hbm, house_ref), (tri_hbm, tri_ref), (x_hbm, x_ref))
+        )
+    ]
+    for load in loads:
+        load.start()
     barrier = pltpu.get_barrier_semaphore()
     nearest = ((row, col_b, True), (row_x, col, True), (row, col_y, True),
                (row - 2, col, jnp.logical_not(top)), (row + 2, col, jnp.logical_not(bottom)))
@@ -174,7 +183,7 @@
         def _():
             act(remote(
                 turned.at[t, pl.ds(h * half, half)], state.at[slot],
-                tile_send.at[t, h], tile_recv.at[slot], to_row, col,
+                tile_send.at[t, h], tile_recv.at[slot - sweeps + 1], to_row, col,
             ))
 
         if keep:
@@ -379,14 +388,14 @@
         def _():
             remote(
                 state.at[u + sweeps], state.at[u + sweeps], tile_send.at[0, 0],
-                tile_recv.at[u + sweeps], row_x, col,
+                tile_recv.at[u + 1], row_x, col,
             ).wait_recv()
 
         @pl.when(top & (u == 0) & (row != 0))
         def _():
             remote(
                 state.at[sweeps - 1], state.at[sweeps - 1], tile_send.at[0, 0],
-                tile_recv.at[sweeps - 1], row_x, col,
+                tile_recv.at[0], row_x, col,
             ).wait_recv()
 
         @pl.when((u == STRIDE * high) & (low <= high) & jnp.logical_not(top))
@@ -516,12 +525,15 @@
 
         lax.fori_loop(low, high, one, 0)
 
+    loads[0].wait()
+    loads[1].wait()
     prepare(0, EARLY)
     pl.semaphore_wait(barrier, greeted)
     greet(heard)
     begin_sweeps(0, EARLY)
     prepare(EARLY, sweeps)
     begin_sweeps(EARLY, sweeps)
+    loads[2].wait()
     for t in range(per):
         turned[t] = x_ref[pl.ds(t * span, span), :].T
 
@@ -596,9 +608,13 @@
     return pl.pallas_call(
         functools.partial(kernel, rows_n, cols_n),
         out_shape=jax.ShapeDtypeStruct((height, columns), jnp.float32),
-        in_specs=[smem, smem, vmem, vmem, vmem],
+        in_specs=[smem, smem] + [pl.BlockSpec(memory_space=pl.ANY)] * 3,
         out_specs=vmem,
         scratch_shapes=[
+            pltpu.VMEM((height, columns), jnp.float32),
+            pltpu.VMEM((sweeps, 1, width, span), jnp.float32),
+            pltpu.VMEM((sweeps, 1, width, width), jnp.float32),
+            dma((3,)),
             pltpu.VMEM((count + sweeps, 2, span, span), jnp.float32),
             pltpu.VMEM((count, 2 * span, 2 * span), jnp.bfloat16),
             pltpu.VMEM((count, 2 * span, 2 * span), jnp.bfloat16),
@@ -610,7 +626,7 @@
             dma((sweeps,)),
             dma((sweeps,)),
             dma((per, 2)),
-            dma((slots,)),
+            dma((widest + 1,)),
             dma((sweeps,)),
             dma((sweeps,)),
             dma((widest,)),

time: 48.8 us -> 48.8 us (level)
  no operation moved by 1% of the time
where the time goes in v4:
time: 48.8 us; the launch traced here: 48.5 us
  Pallas kernels  46.9 us (96%)
  local copies, waits for them, and re-layouts  1.57 us (3%)
    pallas_call x1, Pallas kernels, local(): pl.pallas_call(functools.partial(kernel, rows_n, cols_n), out_shape=jax.S...  46.9 us
    unnamed x1, local copies, waits for them, and re-layouts  1.57 us

profile of v4, /device:TPU:18, one launch (start us, length us, event | category | flops | bytes accessed | tf_op | source)
XLA Modules:
  0.0 48.5 jit_solution(10464426893685405967)
XLA Ops:
  0.0 46.9 %shard_map.55 = f32[256,128]{1,0:T(8,128)} custom-call(s32[8]{0:T(128)} %order_ref.1, s32[8]{0:T(128)} %off_ref.1, f32[256,128]{1,0:T(8,128)} %x_hbm.1, f32[8,1,64,128]{3,2,1,0:T(8,128)} %bitcast.1, f32[8,1,64,64]{3,2,1,0:T(8,128)} %tri_hbm.1), custom_call_target="tpu_custom_call" | custom-call | tf_op jit(solution)/shard_map/pallas_call | solution.py:608
  46.9 1.6 %copy.7 = f32[256,128]{1,0:T(8,128)} copy(f32[256,128]{1,0:T(8,128)} %shard_map.55) | data formatting | bytes 262144
